TPU v7x, 128 devices: a whole 4x4x4 slice. The times are simulated.
128 devices in a mesh: own: 32 (over x, z, core), rep: 4 (over y).
Axes of the slice: x: 4, y: 4, z: 4, core: 2. Of those that a mesh axis runs over, the one named last changes fastest.
Arguments:
- block_pool: bfloat16 [8192, 64, 576], P(('own', 'rep')), may hold values from -16 to 16
- sel_index: int32 [4096], P(('own', 'rep')), may hold values from 0 to 63
- sel_layer: int32 [4096], P(('own', 'rep')), may hold values from 0 to 15, as said below
- counts: int32 [128], P(('own', 'rep')), may hold values from 8 to 32, as said below
Outputs:
- quant_codes: bfloat16 [32, 4, 32, 8, 18432], P('own', 'rep')
- quant_steps: float32 [32, 288], P('own')
- clip_error: float32 [32, 288], P('own')
Inputs may be any that keep to these rules, and one draw needn't show every extreme that they name: `sel_layer`: among the 32 entries of one device, at most 8 name any one layer; the first 8 entries of every device all name one and the same layer. `counts`: some device has all 32 entries live.
All inputs are finite; a program needn't handle non-finite values.
Results may differ from a plain program's by a relative error of at most 0.001.
Values may be sent and summed in bfloat16 or wider, within the bound.
A program may use at most 128 MiB of HBM per device.

v0:
```python
import jax
import jax.numpy as jnp
from jax import lax
from jax.sharding import PartitionSpec as P

SLICES = 2


headroom = 0.5


def sent_to_all(x, axis):
    count = lax.axis_size(axis)
    return lax.all_to_all(jnp.broadcast_to(x[None], (count, *x.shape)), axis, 0, 0, tiled=True)


def of_everyone(x, axis):
    return sent_to_all(x, axis).max(axis=0)


def over_copies(x, axis):
    everything = sent_to_all(x, axis)
    return jnp.sum(everything, axis=0)


def slot_table(index_row, layer_row, live_count, group_layer, capacity):
    n_select = index_row.shape[0]
    is_live = jnp.arange(n_select) < live_count
    matches = (layer_row[None, :] == group_layer[:, None]) & is_live[None, :]
    ranking = jnp.cumsum(matches.astype(jnp.int32), axis=1) - 1
    slot_hit = matches[:, None, :] & (ranking[:, None, :] == jnp.arange(capacity)[None, :, None])
    chosen = jnp.sum(jnp.where(slot_hit, index_row[None, None, :], 0), axis=2)
    filled = jnp.any(slot_hit, axis=2)
    return (chosen, filled)


def body(block_pool, sel_index, sel_layer, counts):
    own_count = lax.axis_size("own")
    rep_count = lax.axis_size("rep")
    n_select = sel_index.shape[0]
    capacity = n_select // 4
    block_tokens = block_pool.shape[1]
    latent_width = block_pool.shape[2]
    half_width = latent_width // SLICES
    flat_width = block_tokens * half_width
    layer_count = own_count // SLICES
    layer_ids = jnp.arange(layer_count)
    chosen, filled = slot_table(sel_index, sel_layer, counts[0], layer_ids, capacity)
    pool_rows = block_pool.reshape(block_pool.shape[0], block_tokens * latent_width)
    picked = jnp.take(pool_rows, chosen.reshape(-1), axis=0)
    picked = jnp.where(filled.reshape(-1)[:, None], picked, jnp.zeros((), picked.dtype))
    picked = picked.reshape(layer_count, capacity, block_tokens, SLICES, half_width)
    parted = picked.transpose(0, 3, 1, 2, 4).reshape(own_count, capacity, flat_width)
    denominator = float(own_count * rep_count * capacity * block_tokens)
    arrived = lax.all_to_all(parted, "own", split_axis=0, concat_axis=0, tiled=True)
    flat_peak = jnp.max(jnp.abs(arrived), axis=(0, 1)).astype(jnp.float32)
    local_peak = jnp.max(flat_peak.reshape(block_tokens, half_width), axis=0)
    peak_abs = of_everyone(local_peak, "rep")
    step_size = headroom * jnp.maximum(peak_abs, 1.0) / 127.0
    step_flat = jnp.tile(step_size, block_tokens)
    values = arrived.astype(jnp.float32)
    encoded = jnp.clip(values / step_flat, -127.0, 127.0).astype(jnp.bfloat16)
    encoded = lax.optimization_barrier(encoded)
    decoded = encoded.astype(jnp.float32) * step_flat
    flat_error = jnp.sum((values - decoded) ** 2, axis=(0, 1))
    sq_error = jnp.sum(flat_error.reshape(block_tokens, half_width), axis=0)
    error_all = over_copies(sq_error, "rep")
    steps_out = step_size[None, :]
    error_out = (error_all / (step_size * step_size * denominator))[None, :]
    return (encoded[None, None], steps_out, error_out)


def solution(mesh):
    return jax.shard_map(
        body,
        mesh=mesh,
        in_specs=(
            P(("own", "rep"), None, None),
            P(("own", "rep")),
            P(("own", "rep")),
            P(("own", "rep")),
        ),
        out_specs=(P("own", "rep", None, None, None), P("own", None), P("own", None)),
        check_vma=False,
    )
```

profile of v0, /device:TPU:0, one launch (start us, length us, event | category | flops | bytes accessed | tf_op | source)
XLA Modules:
  0.0 263.0 jit_solution(13616483861530412258)
XLA Ops:
  1.3 0.7 fusion.7
  2.0 0.2 reduce_window_sum.11
  2.1 0.4 fusion.6
  2.5 1.0 select_reduce_fusion
  3.7 9.9 %reshape.174 = bf16[64,36864]{1,0:T(8,128)(2,1)} reshape(bf16[64,64,576]{2,1,0:T(8,128)(2,1)} %param.4) | data formatting | bytes 9437184 | tf_op jit(solution)/shard_map/reshape | solution.py:49
  13.6 21.4 %gather_fusion = bf16[128,36864]{1,0:T(8,128)(2,1)} fusion(bf16[64,36864]{1,0:T(8,128)(2,1)} %reshape.174, s32[1024]{0:T(1024)S(1)} %pad_clamp_fusion), kind=kCustom, calls=%fused_computation | custom fusion | bytes 18874880 | tf_op jit(solution)/shard_map/jit(_take)/gather | solution.py:50
  35.0 24.6 %gather.7 = bf16[16,8,64,2,288]{4,3,2,1,0:T(2,128)(2,1)} reshape(bf16[128,36864]{1,0:T(8,128)(2,1)} %gather_fusion) | data formatting | bytes 18874368 | tf_op jit(solution)/shard_map/jit(_take)/gather | solution.py:50
  59.6 16.3 %fusion.4 = bf16[16,2,8,64,288]{4,1,3,2,0:T(2,128)(2,1)S(1)} fusion(pred[16,8]{1,0:T(8,128)(4,1)S(1)} %fusion.6, bf16[16,8,64,2,288]{4,3,2,1,0:T(2,128)(2,1)} %gather.7, pred[16,8]{1,0:T(8,128)(4,1)S(1)} %compare_and_fusion), kind=kLoop, calls=%fused_computation.9 | loop fusion | flops 9437184 | bytes 18874624 | tf_op jit(solution)/shard_map/transpose | solution.py:53
  75.9 6.8 %copy.10 = bf16[16,2,8,64,288]{4,3,2,1,0:T(8,128)(2,1)} copy(bf16[16,2,8,64,288]{4,1,3,2,0:T(2,128)(2,1)S(1)} %fusion.4) | data formatting | bytes 18874368 | tf_op jit(solution)/shard_map/transpose | solution.py:53
  82.7 20.9 %reshape.176 = bf16[32,8,18432]{2,1,0:T(8,128)(2,1)} reshape(bf16[16,2,8,64,288]{4,3,2,1,0:T(8,128)(2,1)} %copy.10) | data formatting | bytes 18874368 | tf_op jit(solution)/shard_map/reshape | solution.py:53
  103.6 114.9 %all_to_all.17 = bf16[32,8,18432]{2,1,0:T(8,128)(2,1)S(1)} all-to-all(bf16[32,8,18432]{2,1,0:T(8,128)(2,1)} %reshape.176), channel_id=1, replica_groups=mesh['own'=32,'rep'=4] {'own'}, dimensions={0} | all-to-all | bytes 18874368 | tf_op jit(solution)/shard_map/all_to_all | solution.py:55
  218.6 3.6 %copy-done = bf16[32,8,18432]{2,1,0:T(8,128)(2,1)} copy-done((bf16[32,8,18432]{2,1,0:T(8,128)(2,1)}, bf16[32,8,18432]{2,1,0:T(8,128)(2,1)S(1)}, u32[]{:S(2)}) %copy-start) | copy-done | bytes 9437208
  222.2 1.1 abs_reduce_fusion
  223.3 0.1 reduce_max.35
  223.4 9.6 %all_to_all.18 = f32[4,1,288]{2,1,0:T(1,128)S(1)} all-to-all(f32[4,1,288]{2,1,0:T(1,128)S(1)} %broadcast_in_dim.64), channel_id=1, replica_groups=mesh['own'=32,'rep'=4] {'rep'}, dimensions={0} | all-to-all | bytes 9216 | tf_op jit(solution)/shard_map/all_to_all | solution.py:14
  233.1 0.1 div.30
  233.2 9.8 %fusion.1 = bf16[32,8,18432]{2,1,0:T(8,128)(2,1)} fusion(bf16[32,8,18432]{2,1,0:T(8,128)(2,1)} %copy-done, f32[18432]{0:T(1024)S(1)} %div.30), kind=kLoop, calls=%fused_computation.6 | loop fusion | flops 18874368 | bytes 18948096 | tf_op jit(solution)/shard_map/convert_element_type | solution.py:62
  243.0 10.1 %fusion.3 = f32[18432]{0:T(1024)S(1)} fusion(bf16[32,8,18432]{2,1,0:T(8,128)(2,1)} %copy-done, bf16[32,8,18432]{2,1,0:T(8,128)(2,1)} %fusion.1, f32[18432]{0:T(1024)S(1)} %div.30), kind=kLoop, calls=%fused_computation.8 | loop fusion | flops 28293120 | bytes 19021824 | tf_op jit(solution)/shard_map/reduce_sum | solution.py:65
  253.2 0.1 reshape.177
  253.3 0.6 broadcast_in_dim.66
  253.9 3.2 %all-to-all-start.2 = ((f32[4,1,288]{2,1,0:T(1,128)}), f32[4,1,288]{2,1,0:T(1,128)S(1)}, u32[]{:S(2)}, u32[]{:S(2)}) async-start(f32[4,1,288]{2,1,0:T(1,128)} %broadcast_in_dim.66), calls=%async_computation.2 | async-start | bytes 12288 | tf_op jit(solution)/shard_map/all_to_all | solution.py:14
  257.1 0.6 div.33
  257.7 4.7 %all-to-all-done.2 = f32[4,1,288]{2,1,0:T(1,128)S(1)} async-done(((f32[4,1,288]{2,1,0:T(1,128)}), f32[4,1,288]{2,1,0:T(1,128)S(1)}, u32[]{:S(2)}, u32[]{:S(2)}) %all-to-all-start.2) | async-done | bytes 4640 | tf_op jit(solution)/shard_map/all_to_all | solution.py:14
  262.4 0.6 multiply_divide_fusion
  (14 shorter events, 0.3 us)
Async XLA Ops:
  218.6 3.6 %copy-start = (bf16[32,8,18432]{2,1,0:T(8,128)(2,1)}, bf16[32,8,18432]{2,1,0:T(8,128)(2,1)S(1)}, u32[]{:S(2)}) copy-start(bf16[32,8,18432]{2,1,0:T(8,128)(2,1)S(1)} %all_to_all.17) | copy-start | bytes 28311556
  253.9 8.5 %all-to-all-start.2 = ((f32[4,1,288]{2,1,0:T(1,128)}), f32[4,1,288]{2,1,0:T(1,128)S(1)}, u32[]{:S(2)}, u32[]{:S(2)}) async-start(f32[4,1,288]{2,1,0:T(1,128)} %broadcast_in_dim.66), calls=%async_computation.2 | async-start | bytes 12288 | tf_op jit(solution)/shard_map/all_to_all | solution.py:14
where the time goes:
time: 264 us; the launch traced here: 263 us
  blocking collectives  125 us (47%)
  local copies, waits for them, and re-layouts  88.9 us (34%)
  other arithmetic  40.3 us (15%)
  waiting for transfers between devices  4.71 us (2%)
  starting transfers between devices  3.25 us (1%)
    all_to_all x1, blocking collectives, body(): lax.all_to_all(parted, 'own', split_axis=0, concat_axis=0, tiled=True)  115 us
    gather x2, local copies, waits for them, and re-layouts, body(): picked = jnp.take(pool_rows, chosen.reshape(-1), axis=0)  46 us
    reshape x1, local copies, waits for them, and re-layouts, body(): picked.transpose(0, 3, 1, 2, 4).reshape(own_count, capacity, flat_width)  20.9 us
    transpose x1, other arithmetic, body(): picked.transpose(0, 3, 1, 2, 4).reshape(own_count, capacity, flat_width)  16.3 us
    reduce_sum x1, other arithmetic, body(): flat_error = jnp.sum((values - decoded) ** 2, axis=(0, 1))  10.1 us
    reshape x1, local copies, waits for them, and re-layouts, body(): block_pool.reshape(block_pool.shape[0], block_tokens * latent_width)  9.91 us
    convert_element_type x1, other arithmetic, body(): encoded = jnp.clip(values / step_flat, -127.0, 127.0).astype(jnp.bfloat16)  9.83 us
    all_to_all x1, blocking collectives, sent_to_all(): lax.all_to_all(jnp.broadcast_to(x[None], (count, *x.shape)), axis, 0, 0,...  9.57 us
  transfers between devices with their start and end apart: 1, of which 1 were waited for; matrix products, arithmetic and copies ran while one was open for 0% of the time, Pallas kernels for 0%

commit v1 on v0

v1 whole, which is shorter than its diff:
```python
import functools

import jax
import jax.numpy as jnp
from jax import lax
from jax.experimental import pallas as pl
from jax.experimental.pallas import tpu as pltpu
from jax.sharding import PartitionSpec as P

SLICES = 2
HEADROOM = 0.5
MESH = pl.DeviceIdType.MESH


def part_kernel(layers, capacity, half, idx_ref, lay_ref, cnt_ref, pool_ref, out_ref,
                blocks, wide, stage, zeros, slot_of, in_sem, out_sem, zero_sem):
    n_select = idx_ref.shape[0]
    tokens = blocks.shape[1]
    latent = blocks.shape[2]
    for j in range(n_select):
        pltpu.make_async_copy(pool_ref.at[idx_ref[j]], blocks.at[j], in_sem).start()
    live = cnt_ref[0]

    def clear(i, _):
        slot_of[i] = -1
        return 0

    lax.fori_loop(0, layers * capacity + layers, clear, 0)

    def place(j, _):
        layer = lay_ref[j]

        @pl.when(j < live)
        def _():
            rank = slot_of[layers * capacity + layer] + 1
            slot_of[layers * capacity + layer] = rank
            slot_of[layer * capacity + rank] = j
        return 0

    lax.fori_loop(0, n_select, place, 0)
    zeros[...] = jnp.zeros_like(zeros)
    pltpu.make_async_copy(pool_ref.at[pl.ds(0, n_select)], blocks, in_sem).wait()

    def one_layer(layer, used):
        some = slot_of[layers * capacity + layer] >= 0

        @pl.when(jnp.logical_not(some))
        def _():
            cp = pltpu.make_async_copy(zeros, out_ref.at[pl.ds(layer * SLICES, SLICES)], zero_sem)
            cp.start()
            cp.wait()

        @pl.when(some)
        def _():
            @pl.when(used > 0)
            def _():
                pltpu.make_async_copy(stage.at[0], out_ref.at[pl.ds(0, SLICES)], out_sem).wait()
            for c in range(capacity):
                j = slot_of[layer * capacity + c]

                @pl.when(j >= 0)
                def _():
                    for k in range(wide.shape[0]):
                        cols = min(128, latent - k * 128)
                        wide[k, pl.ds(c * tokens, tokens), :cols] = blocks[j, :, k * 128:k * 128 + cols].astype(jnp.float32)

                @pl.when(j < 0)
                def _():
                    wide[:, pl.ds(c * tokens, tokens), :] = jnp.zeros((wide.shape[0], tokens, 128), jnp.float32)

            def four(q, _):
                rows = [jnp.concatenate([wide[k, pl.ds(4 * q + m, capacity, stride=tokens), :]
                                         for k in range(wide.shape[0])], axis=1) for m in range(4)]
                for h in range(SLICES):
                    flat = jnp.concatenate([r[:, h * half:(h + 1) * half] for r in rows], axis=1)
                    stage[0, h, :, pl.ds(pl.multiple_of(q * 4 * half, 128), 4 * half)] = flat.astype(jnp.bfloat16)
                return 0

            lax.fori_loop(0, tokens // 4, four, 0)
            pltpu.make_async_copy(stage.at[0], out_ref.at[pl.ds(layer * SLICES, SLICES)], out_sem).start()
        return used + some.astype(jnp.int32)

    used = lax.fori_loop(0, layers, one_layer, 0)

    @pl.when(used > 0)
    def _():
        pltpu.make_async_copy(stage.at[0], out_ref.at[pl.ds(0, SLICES)], out_sem).wait()


def part(block_pool, sel_index, sel_layer, counts, layers, capacity):
    rows, tokens, latent = block_pool.shape
    half = latent // SLICES
    n_select = sel_index.shape[0]
    groups = layers * SLICES
    smem = pl.BlockSpec(memory_space=pltpu.SMEM)
    return pl.pallas_call(
        functools.partial(part_kernel, layers, capacity, half),
        out_shape=jax.ShapeDtypeStruct((groups, capacity, tokens * half), jnp.bfloat16),
        in_specs=[smem, smem, smem, pl.BlockSpec(memory_space=pltpu.HBM)],
        out_specs=pl.BlockSpec(memory_space=pltpu.HBM),
        scratch_shapes=[
            pltpu.VMEM((n_select, tokens, latent), jnp.bfloat16),
            pltpu.VMEM((-(-latent // 128), capacity * tokens, 128), jnp.float32),
            pltpu.VMEM((1, SLICES, capacity, tokens * half), jnp.bfloat16),
            pltpu.VMEM((SLICES, capacity, tokens * half), jnp.bfloat16),
            pltpu.SMEM((layers * capacity + layers,), jnp.int32),
            pltpu.SemaphoreType.DMA,
            pltpu.SemaphoreType.DMA,
            pltpu.SemaphoreType.DMA,
        ],
    )(sel_index, sel_layer, counts, block_pool)


def rep_peers():
    me = lax.axis_index("rep")
    count = lax.axis_size("rep")
    return [lax.rem(me + d, count) for d in range(1, count)]


def greet():
    barrier = pltpu.get_barrier_semaphore()
    for peer in rep_peers():
        pl.semaphore_signal(barrier, inc=1, device_id={"rep": peer}, device_id_type=MESH)


def share(mine, theirs, send_sem, recv_sem):
    pl.semaphore_wait(pltpu.get_barrier_semaphore(), len(rep_peers()))
    copies = []
    for i, peer in enumerate(rep_peers()):
        cp = pltpu.make_async_remote_copy(
            src_ref=mine, dst_ref=theirs.at[i], send_sem=send_sem.at[i], recv_sem=recv_sem.at[i],
            device_id={"rep": peer}, device_id_type=MESH)
        cp.start()
        copies.append(cp)
    for cp in copies:
        cp.wait()


def peak_kernel(steps, period, x_ref, out_ref, acc, mine, theirs, send_sem, recv_sem):
    i = pl.program_id(0)

    @pl.when(i == 0)
    def _():
        greet()
        acc[...] = jnp.zeros_like(acc)

    def fold(g, top):
        chunk = x_ref[:, :, pl.ds(pl.multiple_of(g * period, 128), period)].astype(jnp.float32)
        return jnp.maximum(top, jnp.max(jnp.abs(chunk), axis=0))

    acc[...] = lax.fori_loop(0, x_ref.shape[2] // period, fold, acc[...])

    @pl.when(i == steps - 1)
    def _():
        mine[...] = jnp.broadcast_to(jnp.max(acc[...], axis=0, keepdims=True), mine.shape)
        share(mine, theirs, send_sem, recv_sem)
        out_ref[...] = jnp.maximum(jnp.max(theirs[...], axis=0), mine[...])


def peaks(arrived, period, per_step=4):
    sources, capacity, flat = arrived.shape
    steps = sources // per_step
    peers = lax.axis_size("rep") - 1
    return pl.pallas_call(
        functools.partial(peak_kernel, steps, period),
        grid=(steps,),
        out_shape=jax.ShapeDtypeStruct((8, period), jnp.float32),
        in_specs=[pl.BlockSpec((per_step, capacity, flat), lambda i: (i, 0, 0))],
        out_specs=pl.BlockSpec((8, period), lambda i: (0, 0)),
        scratch_shapes=[
            pltpu.VMEM((capacity, period), jnp.float32),
            pltpu.VMEM((8, period), jnp.float32),
            pltpu.VMEM((peers, 8, period), jnp.float32),
            pltpu.SemaphoreType.DMA((peers,)),
            pltpu.SemaphoreType.DMA((peers,)),
        ],
        compiler_params=pltpu.CompilerParams(collective_id=0, has_side_effects=True),
    )(arrived)


def code_kernel(period, x_ref, step_ref, out_ref, err_ref):
    @pl.when(pl.program_id(0) == 0)
    def _():
        err_ref[...] = jnp.zeros_like(err_ref)

    step = jnp.broadcast_to(step_ref[...], err_ref.shape)
    inverse = 1.0 / step

    def fold(g, total):
        at = pl.ds(pl.multiple_of(g * period, 128), period)
        for s in range(x_ref.shape[0]):
            values = x_ref[s, :, at].astype(jnp.float32)
            codes = jnp.clip(values * inverse, -127.0, 127.0).astype(jnp.bfloat16)
            out_ref[s, :, at] = codes
            miss = values - codes.astype(jnp.float32) * step
            total = total + miss * miss
        return total

    err_ref[...] = lax.fori_loop(0, x_ref.shape[2] // period, fold, err_ref[...])


def encode(arrived, step_row, period, per_step=4):
    sources, capacity, flat = arrived.shape
    return pl.pallas_call(
        functools.partial(code_kernel, period),
        grid=(sources // per_step,),
        out_shape=(jax.ShapeDtypeStruct(arrived.shape, jnp.bfloat16),
                   jax.ShapeDtypeStruct((capacity, period), jnp.float32)),
        in_specs=[pl.BlockSpec((per_step, capacity, flat), lambda i: (i, 0, 0)),
                  pl.BlockSpec((1, period), lambda i: (0, 0))],
        out_specs=(pl.BlockSpec((per_step, capacity, flat), lambda i: (i, 0, 0)),
                   pl.BlockSpec((capacity, period), lambda i: (0, 0))),
    )(arrived, step_row)


def total_kernel(err_ref, out_ref, mine, theirs, send_sem, recv_sem):
    greet()
    mine[...] = jnp.broadcast_to(jnp.sum(err_ref[...], axis=0, keepdims=True), mine.shape)
    share(mine, theirs, send_sem, recv_sem)
    out_ref[...] = jnp.sum(theirs[...], axis=0) + mine[...]


def totals(err):
    period = err.shape[1]
    peers = lax.axis_size("rep") - 1
    vmem = pl.BlockSpec(memory_space=pltpu.VMEM)
    return pl.pallas_call(
        total_kernel,
        out_shape=jax.ShapeDtypeStruct((8, period), jnp.float32),
        in_specs=[vmem],
        out_specs=vmem,
        scratch_shapes=[
            pltpu.VMEM((8, period), jnp.float32),
            pltpu.VMEM((peers, 8, period), jnp.float32),
            pltpu.SemaphoreType.DMA((peers,)),
            pltpu.SemaphoreType.DMA((peers,)),
        ],
        compiler_params=pltpu.CompilerParams(collective_id=1, has_side_effects=True),
    )(err)


def body(block_pool, sel_index, sel_layer, counts):
    own_count = lax.axis_size("own")
    rep_count = lax.axis_size("rep")
    capacity = sel_index.shape[0] // 4
    tokens = block_pool.shape[1]
    half = block_pool.shape[2] // SLICES
    period = 4 * half
    parted = part(block_pool, sel_index, sel_layer, counts, own_count // SLICES, capacity)
    denominator = float(own_count * rep_count * capacity * tokens)
    arrived = lax.all_to_all(parted, "own", split_axis=0, concat_axis=0, tiled=True)
    top = jnp.max(peaks(arrived, period)[0].reshape(4, half), axis=0)
    step = HEADROOM * jnp.maximum(top, 1.0) / 127.0
    codes, err = encode(arrived, jnp.tile(step, 4)[None, :], period)
    error = jnp.sum(totals(err)[0].reshape(4, half), axis=0)
    return codes[None, None], step[None, :], (error / (step * step * denominator))[None, :]


def solution(mesh):
    return jax.shard_map(
        body,
        mesh=mesh,
        in_specs=(
            P(("own", "rep"), None, None),
            P(("own", "rep")),
            P(("own", "rep")),
            P(("own", "rep")),
        ),
        out_specs=(P("own", "rep", None, None, None), P("own", None), P("own", None)),
        check_vma=False,
    )
```

time: 264 us -> 198 us (0.75)
  local copies, waits for them, and re-layouts: 88.9 us -> 2.98 us
  Pallas kernels: 0 us -> 52.1 us
  other arithmetic: 40.3 us -> 0.63 us
  blocking collectives: 125 us -> 139 us
  waiting for transfers between devices: 4.71 us -> 0 us
  starting transfers between devices: 3.25 us -> 0 us
    pallas_call x0 -> x4, Pallas kernels: none -> 52.1 us  [the longest x1 16.8 us: part(): pl.pallas_call(functools.partial(part_kernel, layers, capacity, half), ou...]
    gather x2 -> x0, local copies, waits for them, and re-layouts: 46 us -> none  [body(): picked = jnp.take(pool_rows, chosen.reshape(-1), axis=0)]
    reshape x4 -> x0, local copies, waits for them, and re-layouts: 31 us -> none  [the longest x1 20.9 us: body(): picked.transpose(0, 3, 1, 2, 4).reshape(own_count, capacity, flat_width)]
    all_to_all x1, blocking collectives: 115 us -> 139 us  [body(): lax.all_to_all(parted, 'own', split_axis=0, concat_axis=0, tiled=True)]
    transpose x1 -> x0, other arithmetic: 16.3 us -> none  [body(): picked.transpose(0, 3, 1, 2, 4).reshape(own_count, capacity, flat_width)]
    reduce_sum x4 -> x1, other arithmetic: 11.2 us -> 0.02 us  [body(): error = jnp.sum(totals(err)[0].reshape(4, half), axis=0)]
    convert_element_type x1 -> x0, other arithmetic: 9.83 us -> none  [body(): encoded = jnp.clip(values / step_flat, -127.0, 127.0).astype(jnp.bfloat16)]
    all_to_all x1 -> x0, blocking collectives: 9.57 us -> none  [sent_to_all(): lax.all_to_all(jnp.broadcast_to(x[None], (count, *x.shape)), axis, 0, 0,...]
  transfers between devices with their start and end apart: 1 -> 0, of which waited for: 1 -> 0; matrix products, arithmetic and copies ran while one was open for 0% -> 0% of each run, Pallas kernels for 0% -> 0%
where the time goes in v1:
time: 198 us; the launch traced here: 197 us
  blocking collectives  139 us (70%)
  Pallas kernels  52.1 us (26%)
  local copies, waits for them, and re-layouts  2.98 us (2%)
    all_to_all x1, blocking collectives, body(): lax.all_to_all(parted, 'own', split_axis=0, concat_axis=0, tiled=True)  139 us
    pallas_call x1, Pallas kernels, part(): pl.pallas_call(functools.partial(part_kernel, layers, capacity, half), ou...  16.8 us
    pallas_call x1, Pallas kernels, peaks(): pl.pallas_call(functools.partial(peak_kernel, steps, period), grid=(steps...  16 us
    pallas_call x1, Pallas kernels, encode(): pl.pallas_call(functools.partial(code_kernel, period), grid=(sources // p...  11.9 us
    pallas_call x1, Pallas kernels, totals(): pl.pallas_call(total_kernel, out_shape=jax.ShapeDtypeStruct((8, period),...  7.41 us

profile of v1, /device:TPU:0, one launch (start us, length us, event | category | flops | bytes accessed | tf_op | source)
XLA Modules:
  0.0 196.5 jit_solution(13909921147501619867)
XLA Ops:
  1.3 16.8 %shard_map.67 = bf16[32,8,18432]{2,1,0:T(8,128)(2,1)} custom-call(s32[32]{0:T(128)} %idx_ref.1, s32[32]{0:T(128)} %lay_ref.1, s32[1]{0:T(128)S(6)} %copy.7.cnt_ref, bf16[64,64,576]{2,1,0:T(8,128)(2,1)} %pool_ref.1), custom_call_target="tpu_custom_call" | custom-call | tf_op jit(solution)/shard_map/pallas_call | solution.py:96
  18.1 139.5 %all_to_all.5.x_ref = bf16[32,8,18432]{2,1,0:T(8,128)(2,1)} all-to-all(bf16[32,8,18432]{2,1,0:T(8,128)(2,1)} %shard_map.67), channel_id=1, replica_groups=mesh['own'=32,'rep'=4] {'own'}, dimensions={0} | all-to-all | bytes 18874368 | tf_op jit(solution)/shard_map/all_to_all | solution.py:251
  157.6 16.0 %shard_map.68 = f32[8,1152]{1,0:T(8,128)} custom-call(bf16[32,8,18432]{2,1,0:T(8,128)(2,1)} %all_to_all.5.x_ref), custom_call_target="tpu_custom_call" | custom-call | tf_op jit(solution)/shard_map/pallas_call | solution.py:164
  173.6 0.8 slice_reduce_fusion.1
  174.4 0.1 reshape_squeeze.6
  174.5 0.6 div.20
  175.1 0.7 broadcast_in_dim_tile.3.step_ref
  175.7 11.9 %shard_map.69 = (bf16[32,8,18432]{2,1,0:T(8,128)(2,1)}, f32[8,1152]{1,0:T(8,128)}) custom-call(bf16[32,8,18432]{2,1,0:T(8,128)(2,1)} %all_to_all.5.x_ref, f32[1,1152]{1,0:T(1,128)} %broadcast_in_dim_tile.3.step_ref), custom_call_target="tpu_custom_call" | custom-call | tf_op jit(solution)/shard_map/pallas_call | solution.py:204
  187.7 7.4 %shard_map.70 = f32[8,1152]{1,0:T(8,128)} custom-call(f32[8,1152]{1,0:T(8,128)} %get-tuple-element.6.err_ref), custom_call_target="tpu_custom_call" | custom-call | tf_op jit(solution)/shard_map/pallas_call | solution.py:227
  195.1 0.8 slice_reduce_fusion
  195.9 0.1 reshape_squeeze.7
  196.0 0.6 multiply_divide_fusion
  (4 shorter events, 0.1 us)

commit v2 on v1

--- a/solution.py
+++ b/solution.py
@@ -213,47 +213,666 @@
     )(arrived, step_row)
 
 
-def total_kernel(err_ref, out_ref, mine, theirs, send_sem, recv_sem):
+def total_kernel(denominator, err_ref, step_ref, out_ref, mine, theirs, send_sem, recv_sem):
     greet()
-    mine[...] = jnp.broadcast_to(jnp.sum(err_ref[...], axis=0, keepdims=True), mine.shape)
+    half = step_ref.shape[1]
+    row = jnp.sum(err_ref[...], axis=0, keepdims=True)
+    parts = [row[:, m * half:(m + 1) * half] for m in range(4)]
+    mine[...] = jnp.broadcast_to((parts[0] + parts[1]) + (parts[2] + parts[3]), mine.shape)
     share(mine, theirs, send_sem, recv_sem)
-    out_ref[...] = jnp.sum(theirs[...], axis=0) + mine[...]
-
-
-def totals(err):
-    period = err.shape[1]
+    total = (jnp.sum(theirs[...], axis=0) + mine[...])[0:1]
+    step = step_ref[...]
+    out_ref[...] = total / (step * step * denominator)
+
+
+def totals(err, step, denominator):
+    half = step.shape[1]
     peers = lax.axis_size("rep") - 1
     vmem = pl.BlockSpec(memory_space=pltpu.VMEM)
     return pl.pallas_call(
-        total_kernel,
-        out_shape=jax.ShapeDtypeStruct((8, period), jnp.float32),
-        in_specs=[vmem],
+        functools.partial(total_kernel, denominator),
+        out_shape=jax.ShapeDtypeStruct((1, half), jnp.float32),
+        in_specs=[vmem, vmem],
         out_specs=vmem,
         scratch_shapes=[
-            pltpu.VMEM((8, period), jnp.float32),
-            pltpu.VMEM((peers, 8, period), jnp.float32),
+            pltpu.VMEM((8, half), jnp.float32),
+            pltpu.VMEM((peers, 8, half), jnp.float32),
             pltpu.SemaphoreType.DMA((peers,)),
             pltpu.SemaphoreType.DMA((peers,)),
         ],
         compiler_params=pltpu.CompilerParams(collective_id=1, has_side_effects=True),
-    )(err)
+    )(err, step)
+
+
+SIDE = 4
+CAP_ONE = 20
+CAP_TWO = 16
+BY_LAYER, BY_SIDE, LIVE = 32, 48, 56
+
+
+def open_kernel(half, idx_ref, lay_ref, cnt_ref, pool_ref, hot_ref, cold_ref, table_ref,
+                pool, wide, flat, row_ref, pool_sem, own_send, own_recv, send_sem, recv_sem):
+    n_select = idx_ref.shape[0]
+    tokens, latent = pool.shape[1], pool.shape[2]
+    capacity = hot_ref.shape[1]
+    tiles = wide.shape[0]
+    fetch = pltpu.make_async_copy(pool_ref, pool, pool_sem)
+    fetch.start()
+    me, mine = lax.axis_index("own"), lax.axis_index("rep")
+    owners = lax.axis_size("own")
+    barrier = pltpu.get_barrier_semaphore()
+
+    def hello(i, _):
+        pl.semaphore_signal(barrier, inc=1, device_id={"own": lax.rem(me + i, owners)}, device_id_type=MESH)
+        return 0
+
+    lax.fori_loop(1, owners, hello, 0)
+    greet()
+
+    lane = lax.broadcasted_iota(jnp.int32, (1, 128), 1)
+    live = cnt_ref[0]
+    row = jnp.where(lane == LIVE, live, jnp.where(lane < BY_LAYER, -1, 0))
+    for j in range(n_select):
+        layer = lay_ref[j]
+        is_live = jnp.where(j < live, 1, 0)
+        row = jnp.where(lane == j, jnp.where(j < live, layer, -1), row)
+        if j >= capacity:
+            spot = ((lane == BY_LAYER + layer) | (lane == BY_SIDE + lax.shift_right_logical(layer, 2))
+                    | (lane == BY_SIDE + SIDE + (layer & (SIDE - 1))))
+            row = row + jnp.where(spot, is_live, 0)
+    row_ref[...] = row
+    table_ref[mine, me] = row
+    pl.semaphore_wait(barrier, owners - 1 + len(rep_peers()))
+
+    def push(i, _):
+        pltpu.make_async_remote_copy(
+            src_ref=row_ref, dst_ref=table_ref.at[mine, me], send_sem=own_send, recv_sem=own_recv,
+            device_id={"own": lax.rem(me + i, owners)}, device_id_type=MESH).start()
+        return 0
+
+    lax.fori_loop(1, owners, push, 0)
+    fetch.wait()
+
+    def widen(j, to):
+        at = idx_ref[j]
+        for k in range(tiles):
+            cols = min(128, latent - k * 128)
+            wide[k, pl.ds(to, tokens), :cols] = pool[at, :, k * 128:k * 128 + cols].astype(jnp.float32)
+
+    def strided(start, count, stride):
+        return jnp.concatenate([wide[k, pl.ds(start, count, stride=stride), :] for k in range(tiles)], axis=1)
+
+    for c in range(capacity):
+        widen(c, c * tokens)
+
+    def four(q, _):
+        rows = [strided(4 * q + m, capacity, tokens) for m in range(4)]
+        for h in range(SLICES):
+            line = jnp.concatenate([r[:, h * half:(h + 1) * half] for r in rows], axis=1)
+            hot_ref[h, :, pl.ds(pl.multiple_of(q * 4 * half, 128), 4 * half)] = line.astype(jnp.bfloat16)
+        return 0
+
+    lax.fori_loop(0, tokens // 4, four, 0)
+
+    rest = table_ref.at[mine, pl.ds(0, owners - 1)]
+    pltpu.make_async_copy(rest, rest, own_recv).wait()
+    pltpu.make_async_copy(rest, rest, own_send).wait()
+    copies = []
+    for i, peer in enumerate(rep_peers()):
+        cp = pltpu.make_async_remote_copy(
+            src_ref=table_ref.at[mine], dst_ref=table_ref.at[mine], send_sem=send_sem.at[i], recv_sem=recv_sem.at[i],
+            device_id={"rep": peer}, device_id_type=MESH)
+        cp.start()
+        copies.append(cp)
+
+    quads = tokens // 4
+    lines = 4 * half // 128
+
+    def one(j, _):
+        widen(j, 0)
+        rows = [strided(m, quads, 4) for m in range(4)]
+        for h in range(SLICES):
+            line = jnp.concatenate([r[:, h * half:(h + 1) * half] for r in rows], axis=1)
+            for i in range(lines):
+                flat[h, pl.ds(i, quads, stride=lines), :] = line[:, i * 128:(i + 1) * 128]
+        for h in range(SLICES):
+            cold_ref[h, j - capacity] = flat[h].astype(jnp.bfloat16)
+        return 0
+
+    lax.fori_loop(capacity, n_select, one, 0)
+    for cp in copies:
+        cp.wait()
+
+
+def open_exchange(block_pool, sel_index, sel_layer, counts, capacity):
+    _, tokens, latent = block_pool.shape
+    half = latent // SLICES
+    n_select = sel_index.shape[0]
+    lines = tokens * half // 128
+    owners, reps = lax.axis_size("own"), lax.axis_size("rep")
+    smem = pl.BlockSpec(memory_space=pltpu.SMEM)
+    vmem = pl.BlockSpec(memory_space=pltpu.VMEM)
+    return pl.pallas_call(
+        functools.partial(open_kernel, half),
+        out_shape=(jax.ShapeDtypeStruct((SLICES, capacity, tokens * half), jnp.bfloat16),
+                   jax.ShapeDtypeStruct((SLICES, n_select - capacity, lines, 128), jnp.bfloat16),
+                   jax.ShapeDtypeStruct((reps, owners, 1, 128), jnp.int32)),
+        in_specs=[smem, smem, smem, pl.BlockSpec(memory_space=pltpu.HBM)],
+        out_specs=(vmem, vmem, vmem),
+        scratch_shapes=[
+            pltpu.VMEM(block_pool.shape, jnp.bfloat16),
+            pltpu.VMEM((-(-latent // 128), capacity * tokens, 128), jnp.float32),
+            pltpu.VMEM((SLICES, lines, 128), jnp.float32),
+            pltpu.VMEM((1, 128), jnp.int32),
+            pltpu.SemaphoreType.DMA,
+            pltpu.SemaphoreType.DMA,
+            pltpu.SemaphoreType.DMA,
+            pltpu.SemaphoreType.DMA((reps - 1,)),
+            pltpu.SemaphoreType.DMA((reps - 1,)),
+        ],
+        compiler_params=pltpu.CompilerParams(collective_id=2, has_side_effects=True),
+    )(sel_index, sel_layer, counts, block_pool)
+
+
+def place():
+    me = lax.axis_index("own")
+    core = lax.rem(me, 2)
+    x, z = me // (2 * SIDE), lax.rem(me // 2, SIDE)
+    return core, jnp.where(core == 0, x, z), jnp.where(core == 0, z, x)
+
+
+def index_of(core, a, b, slot):
+    return jnp.where(core == 0, a * SIDE + b, b * SIDE + a) * 2 + slot
+
+
+def chip_peer(core, a, b, slot):
+    return {"own": index_of(core, lax.rem(a, SIDE), lax.rem(b, SIDE), slot)}
+
+
+def plan_kernel(capacity, n_cold, table_ref, rows_ref, fits_ref, one_ref, two_ref, number_ref, where_ref, flag_ref,
+                near, rank_one, rank_two, sem):
+    core, a, b = place()
+    me = lax.axis_index("own")
+    cp = pltpu.make_async_copy(rows_ref.at[lax.axis_index("rep")], near, sem)
+    cp.start()
+    reps, owners = table_ref.shape[0], table_ref.shape[1]
+    lane = lax.broadcasted_iota(jnp.int32, (1, 128), 1)
+    one, two = jnp.zeros((1, 128), jnp.int32), jnp.zeros((1, 128), jnp.int32)
+    for r in range(reps):
+        chips = [table_ref[r, 2 * c] + table_ref[r, 2 * c + 1] for c in range(SIDE * SIDE)]
+        for c in chips:
+            one = jnp.maximum(one, c)
+        for i in range(SIDE):
+            for picked in (chips[i::SIDE], chips[SIDE * i:SIDE * i + SIDE]):
+                two = jnp.maximum(two, (picked[0] + picked[1]) + (picked[2] + picked[3]))
+    one = jnp.where((lane >= BY_SIDE) & (lane < LIVE), one, 0).astype(jnp.float32)
+    two = jnp.where((lane >= BY_LAYER) & (lane < BY_SIDE), two, 0).astype(jnp.float32)
+    fits_ref[0] = jnp.where(jnp.logical_and(jnp.max(one) <= CAP_ONE, jnp.max(two) <= CAP_TWO), 1, 0)
+
+    def clear(ref, value):
+        def put(i, _):
+            ref[i] = value
+            return 0
+        lax.fori_loop(0, ref.shape[0], put, 0, unroll=8 if ref.shape[0] % 8 == 0 else 1)
+
+    clear(one_ref, 0)
+    clear(two_ref, 0)
+    clear(number_ref, 0)
+    clear(where_ref, -1)
+    clear(rank_two, 0)
+    cp.wait()
+    layer_here = me // 2
+    flag_ref[0] = jnp.where(near[0, 0, 0] == layer_here, 1, 0)
+
+    def column(a_from, _):
+        clear(rank_one, 0)
+        for slot in range(2):
+            device = index_of(core, a_from, b, slot)
+
+            def entry(j, _):
+                layer = near[device, 0, j]
+                high, low = lax.shift_right_logical(layer, 2), layer & (SIDE - 1)
+                to_a = jnp.where(core == 0, high, low)
+                to_b = jnp.where(core == 0, low, high)
+                first = rank_one[to_a]
+                rank_one[to_a] = first + 1
+                first = jnp.minimum(first, CAP_ONE - 1)
+
+                @pl.when(a_from == a)
+                def _():
+                    one_ref[to_a * CAP_ONE + first] = slot * n_cold + j - capacity
+
+                @pl.when(to_a == a)
+                def _():
+                    second = rank_two[to_b]
+                    rank_two[to_b] = second + 1
+                    two_ref[to_b * CAP_TWO + jnp.minimum(second, CAP_TWO - 1)] = a_from * CAP_ONE + first
+                return 0
+
+            lax.fori_loop(capacity, near[device, 0, LIVE], entry, 0)
+        return 0
+
+    lax.fori_loop(0, SIDE, column, 0)
+
+    def arriving(n, _):
+        b_from, a_from, slot = n // (2 * SIDE), lax.rem(n // 2, SIDE), lax.rem(n, 2)
+        device = index_of(core, a_from, b_from, slot)
+
+        @pl.when(near[device, 0, BY_LAYER + layer_here] > 0)
+        def _():
+            def entry(j, held):
+                hit = near[device, 0, j] == layer_here
+
+                @pl.when(hit)
+                def _():
+                    count = number_ref[b_from]
+                    number_ref[b_from] = count + 1
+                    where_ref[device * capacity + held] = b_from * CAP_TWO + count
+                return held + jnp.where(hit, 1, 0)
+
+            lax.fori_loop(capacity, near[device, 0, LIVE], entry, 0)
+        return 0
+
+    lax.fori_loop(0, owners, arriving, 0)
+
+
+def plan(table, capacity, n_cold):
+    reps, owners = table.shape[0], table.shape[1]
+    smem = pl.BlockSpec(memory_space=pltpu.SMEM)
+    sizes = (1, SIDE * CAP_ONE, SIDE * CAP_TWO, SIDE, owners * capacity, 1)
+    return pl.pallas_call(
+        functools.partial(plan_kernel, capacity, n_cold),
+        out_shape=tuple(jax.ShapeDtypeStruct((n,), jnp.int32) for n in sizes),
+        in_specs=[pl.BlockSpec(memory_space=pltpu.VMEM), pl.BlockSpec(memory_space=pl.ANY)],
+        out_specs=tuple(smem for _ in sizes),
+        scratch_shapes=[
+            pltpu.SMEM((owners, 1, 128), jnp.int32),
+            pltpu.SMEM((SIDE,), jnp.int32),
+            pltpu.SMEM((SIDE,), jnp.int32),
+            pltpu.SemaphoreType.DMA,
+        ],
+    )(table, table)
+
+
+def route_kernel(layer, one_ref, two_ref, number_ref, hot_ref, cold_ref, out_ref, landed, row_ref,
+                 final, held, first, passed, second, acc, flat, mine, theirs,
+                 sem_send, sem_block, sem_out, sems_s, sems_r, local, send_sem, recv_sem):
+    core, a, b = place()
+    me = lax.axis_index("own")
+    other = 1 - core
+    beside = index_of(core, a, b, other)
+    n_cold = cold_ref.shape[1]
+    star_x, star_z = layer // SIDE, layer % SIDE
+    star_a = jnp.where(core == 0, star_x, star_z)
+    star_b = jnp.where(core == 0, star_z, star_x)
+    da = lax.rem(a + SIDE - star_a, SIDE)
+    db = lax.rem(b + SIDE - star_b, SIDE)
+    relay = jnp.logical_and(da == 0, db != 0)
+    star = jnp.logical_and(da == 0, db == 0)
+    barrier = pltpu.get_barrier_semaphore()
+    partner = chip_peer(core, a, b, other)
+    pl.semaphore_signal(barrier, inc=1, device_id=partner, device_id_type=MESH)
+    for d in range(1, SIDE):
+        pl.semaphore_signal(barrier, inc=1, device_id=chip_peer(core, a + d, b, core), device_id_type=MESH)
+        pl.semaphore_signal(barrier, inc=1, device_id=chip_peer(core, a, b + d, core), device_id_type=MESH)
+    greet()
+    keep_hot = pltpu.make_async_copy(hot_ref.at[core], final.at[me], local.at[0])
+    keep_hot.start()
+    keep_cold = pltpu.make_async_copy(cold_ref.at[core], held.at[pl.ds(core * n_cold, n_cold)], local.at[1])
+    keep_cold.start()
+    pl.semaphore_wait(barrier, 2 * SIDE - 1 + len(rep_peers()))
+
+    def send(src, dst, send_at, recv_at, to):
+        return pltpu.make_async_remote_copy(
+            src_ref=src, dst_ref=dst, send_sem=send_at, recv_sem=recv_at, device_id=to, device_id_type=MESH)
+
+    swap_cold = send(cold_ref.at[other], held.at[pl.ds(core * n_cold, n_cold)], sems_s.at[0], sems_r.at[0], partner)
+    swap_cold.start()
+    swap_hot = send(hot_ref.at[other], final.at[me], sem_send.at[0], sem_block.at[me], partner)
+    swap_hot.start()
+    keep_hot.wait()
+
+    dist = jnp.where(da != 0, da, db)
+
+    def onward(slot):
+        step = jnp.where(dist == 2, jnp.where(slot == 0, 1, SIDE - 1), SIDE - dist)
+        return chip_peer(core, a + jnp.where(da != 0, step, 0), b + jnp.where(da != 0, 0, step), core)
+
+    def forward(s, n, slot):
+        send(final.at[s], final.at[s], sem_send.at[n], sem_block.at[s], onward(slot)).start()
+
+    def got(s):
+        pltpu.make_async_copy(final.at[s], final.at[s], sem_block.at[s]).wait()
+
+    @pl.when(jnp.logical_not(star))
+    def _():
+        forward(me, 1, core)
+        got(beside)
+        forward(beside, 2, other)
+
+    keep_cold.wait()
+    swap_cold.wait()
+
+    def pack(src, table, at, dst, start, count):
+        def body(k, _):
+            dst[start + k] = src[table[at + k]]
+            return 0
+        lax.fori_loop(0, count, body, 0)
+
+    copies = []
+    for d in (2, 1, 3):
+        pack(held, one_ref, lax.rem(a + d, SIDE) * CAP_ONE, first, (d - 1) * CAP_ONE, CAP_ONE)
+        cp = send(first.at[pl.ds((d - 1) * CAP_ONE, CAP_ONE)], passed.at[pl.ds(a * CAP_ONE, CAP_ONE)],
+                  sems_s.at[d], sems_r.at[d], chip_peer(core, a + d, b, core))
+        cp.start()
+        copies.append(cp)
+    pack(held, one_ref, a * CAP_ONE, passed, a * CAP_ONE, CAP_ONE)
+
+    @pl.when(jnp.logical_or(da == 1, da == 3))
+    def _():
+        slot = jnp.where(da == 1, 1, 0)
+        s = index_of(core, lax.rem(star_a + 2, SIDE), b, slot)
+        got(s)
+        forward(s, 3, slot)
+
+    for cp in copies:
+        cp.wait()
+    copies = []
+    for d in (2, 1, 3):
+        pack(passed, two_ref, lax.rem(b + d, SIDE) * CAP_TWO, second, (d - 1) * CAP_TWO, CAP_TWO)
+        cp = send(second.at[pl.ds((d - 1) * CAP_TWO, CAP_TWO)], landed.at[pl.ds(b * CAP_TWO, CAP_TWO)],
+                  sems_s.at[SIDE - 1 + d], sems_r.at[SIDE - 1 + d], chip_peer(core, a, b + d, core))
+        cp.start()
+        copies.append(cp)
+    pack(passed, two_ref, b * CAP_TWO, landed, b * CAP_TWO, CAP_TWO)
+
+    def of(a_from, b_from, slot):
+        return index_of(core, lax.rem(star_a + a_from, SIDE), lax.rem(star_b + b_from, SIDE), slot)
+
+    def row_order(p):
+        return jnp.where(p < 2, p, 5 - p)
+
+    @pl.when(relay)
+    def _():
+        def row_block(i, _):
+            slot = lax.rem(i, 2)
+            s = of(row_order(i // 2), db, slot)
+            got(s)
+            forward(s, 1 + i, slot)
+            return 0
+
+        lax.fori_loop(2, 2 * SIDE, row_block, 0)
+
+        @pl.when(db != 2)
+        def _():
+            slot = jnp.where(db == 1, 1, 0)
+
+            def far_block(p, _):
+                s = of(row_order(p), 2, slot)
+                got(s)
+                forward(s, 2 * SIDE + 1 + p, slot)
+                return 0
+
+            lax.fori_loop(0, SIDE, far_block, 0)
+
+    period = acc.shape[1]
+    lines = period // 128
+
+    @pl.when(star)
+    def _():
+        acc[...] = jnp.zeros_like(acc)
+
+        def take(s, n):
+            pltpu.make_async_copy(final.at[s], out_ref.at[s], sem_out.at[n]).start()
+
+            def fold(g, top):
+                chunk = final[s, :, pl.ds(pl.multiple_of(g * period, 128), period)].astype(jnp.float32)
+                return jnp.maximum(top, jnp.abs(chunk))
+
+            acc[...] = lax.fori_loop(0, final.shape[2] // period, fold, acc[...])
+
+        take(me, 0)
+
+        def arrive(n, _):
+            i = n - 2
+            step, which = i // 3, lax.rem(i, 3)
+            early = i < 18
+            row_a = jnp.where(step < 4, 1 + 2 * lax.rem(step, 2), 2)
+            row_slot = jnp.where(step < 4, step // 2, step - 4)
+            near_step = jnp.where(early, step, 6 + (i - 18) // 2)
+            near_b = jnp.where(early, which * 2 - 1, 1 + 2 * lax.rem(i - 18, 2))
+            far_step = i - 22
+            is_row = jnp.logical_and(early, which == 0)
+            is_far = i >= 22
+            block_step = jnp.where(is_far, far_step, near_step)
+            from_a = jnp.where(is_row, row_a, row_order(block_step // 2))
+            from_b = jnp.where(is_row, 0, jnp.where(is_far, 2, near_b))
+            slot = jnp.where(is_row, row_slot, lax.rem(block_step, 2))
+            s = jnp.where(n == 1, beside, of(from_a, from_b, slot))
+            got(s)
+            take(s, n)
+            return 0
+
+        lax.fori_loop(1, 32, arrive, 0)
+
+    for cp in copies:
+        cp.wait()
+
+    @pl.when(jnp.logical_not(star))
+    def _():
+        flat[...] = jnp.zeros_like(flat)
+        for q in range(SIDE):
+            def cold_fold(k, _):
+                block = jnp.abs(landed[q * CAP_TWO + k].astype(jnp.float32))
+                flat[...] = jnp.maximum(flat[...], jnp.where(k < number_ref[q], block, 0.0))
+                return 0
+            lax.fori_loop(0, CAP_TWO, cold_fold, 0)
+        quads = flat.shape[0] // lines
+        row = jnp.concatenate([jnp.max(flat[pl.ds(i, quads, stride=lines), :], axis=0, keepdims=True)
+                               for i in range(lines)], axis=1)
+        acc[...] = jnp.broadcast_to(row, acc.shape)
+
+    half = period // 4
+    top = jnp.max(acc[...], axis=0, keepdims=True)
+    parts = [top[:, m * half:(m + 1) * half] for m in range(4)]
+    peak = jnp.maximum(jnp.maximum(parts[0], parts[1]), jnp.maximum(parts[2], parts[3]))
+    mine[...] = jnp.broadcast_to(peak, mine.shape)
+    swap_hot.wait_send()
+
+    def drained(n, _):
+        pltpu.make_async_copy(final.at[0], final.at[0], sem_send.at[n]).wait()
+        return 0
+
+    sent = jnp.where(da != 0, jnp.where(da == 2, 2, 3), jnp.where(db == 0, 0, jnp.where(db == 2, 8, 12)))
+    lax.fori_loop(1, sent + 1, drained, 0)
+    copies = []
+    for i, peer in enumerate(rep_peers()):
+        cp = send(mine, theirs.at[i], send_sem.at[i], recv_sem.at[i], {"rep": peer})
+        cp.start()
+        copies.append(cp)
+
+    @pl.when(star)
+    def _():
+        def written(n, _):
+            pltpu.make_async_copy(final.at[0], final.at[0], sem_out.at[n]).wait()
+            return 0
+
+        lax.fori_loop(0, 32, written, 0)
+
+    for cp in copies:
+        cp.wait()
+    peak = jnp.maximum(jnp.max(theirs[...], axis=0), mine[...])
+    step = HEADROOM * jnp.maximum(peak, 1.0) / 127.0
+    row_ref[...] = jnp.concatenate([step] * 4, axis=1)
+
+
+def route(layer, one, two, number, hot, cold):
+    _, capacity, flat = hot.shape
+    owners = lax.axis_size("own")
+    peers = lax.axis_size("rep") - 1
+    _, n_cold, lines, width = cold.shape
+    period = flat // 16
+    half = period // 4
+    smem = pl.BlockSpec(memory_space=pltpu.SMEM)
+    vmem = pl.BlockSpec(memory_space=pltpu.VMEM)
+    block, small = (capacity, flat), (lines, width)
+    return pl.pallas_call(
+        functools.partial(route_kernel, layer),
+        out_shape=(jax.ShapeDtypeStruct((owners, *block), hot.dtype),
+                   jax.ShapeDtypeStruct((SIDE * CAP_TWO, *small), cold.dtype),
+                   jax.ShapeDtypeStruct((8, period), jnp.float32)),
+        in_specs=[smem, smem, smem, pl.BlockSpec(memory_space=pl.ANY), pl.BlockSpec(memory_space=pl.ANY)],
+        out_specs=(pl.BlockSpec(memory_space=pltpu.HBM), vmem, vmem),
+        scratch_shapes=[
+            pltpu.VMEM((owners, *block), hot.dtype),
+            pltpu.VMEM((2 * n_cold, *small), cold.dtype),
+            pltpu.VMEM(((SIDE - 1) * CAP_ONE, *small), cold.dtype),
+            pltpu.VMEM((SIDE * CAP_ONE, *small), cold.dtype),
+            pltpu.VMEM(((SIDE - 1) * CAP_TWO, *small), cold.dtype),
+            pltpu.VMEM((capacity, period), jnp.float32),
+            pltpu.VMEM((lines, width), jnp.float32),
+            pltpu.VMEM((8, half), jnp.float32),
+            pltpu.VMEM((peers, 8, half), jnp.float32),
+            pltpu.SemaphoreType.DMA((13,)),
+            pltpu.SemaphoreType.DMA((owners,)),
+            pltpu.SemaphoreType.DMA((owners,)),
+            pltpu.SemaphoreType.DMA((2 * SIDE - 1,)),
+            pltpu.SemaphoreType.DMA((2 * SIDE - 1,)),
+            pltpu.SemaphoreType.DMA((2,)),
+            pltpu.SemaphoreType.DMA((peers,)),
+            pltpu.SemaphoreType.DMA((peers,)),
+        ],
+        compiler_params=pltpu.CompilerParams(collective_id=4 + layer, has_side_effects=True,
+                                             vmem_limit_bytes=50 * 1024 * 1024),
+    )(one, two, number, hot, cold)
+
+
+def finish_kernel(period, flag_ref, where_ref, x_ref, cold_ref, step_ref, out_ref, err_ref, step_out, wide, flat_step, flat_err):
+    i = pl.program_id(0)
+    sources, capacity, width = x_ref.shape
+    lines = period // 128
+    rows = width // 128
+    quads = rows // lines
+    star = flag_ref[0] == 1
+    step_row = step_ref[0:1]
+
+    @pl.when(i == 0)
+    def _():
+        step_out[...] = step_row[:, :step_out.shape[1]]
+        err_ref[...] = jnp.zeros_like(err_ref)
+        flat_err[...] = jnp.zeros_like(flat_err)
+        for k in range(lines):
+            flat_step[pl.ds(k, quads, stride=lines), :] = jnp.broadcast_to(
+                step_row[:, k * 128:(k + 1) * 128], (quads, 128))
+
+    @pl.when(star)
+    def _():
+        step = jnp.broadcast_to(step_row, err_ref.shape)
+        inverse = 1.0 / step
+
+        def fold(g, total):
+            at = pl.ds(pl.multiple_of(g * period, 128), period)
+            for s in range(sources):
+                values = x_ref[s, :, at].astype(jnp.float32)
+                codes = jnp.clip(values * inverse, -127.0, 127.0).astype(jnp.bfloat16)
+                out_ref[s, :, at] = codes
+                miss = values - codes.astype(jnp.float32) * step
+                total = total + miss * miss
+            return total
+
+        err_ref[...] = lax.fori_loop(0, width // period, fold, err_ref[...])
+
+    @pl.when(jnp.logical_not(star))
+    def _():
+        for s in range(sources):
+            base = (i * sources + s) * capacity
+            first = where_ref[base]
+
+            @pl.when(first < 0)
+            def _():
+                out_ref[s] = jnp.zeros((capacity, width), jnp.bfloat16)
+
+            @pl.when(first >= 0)
+            def _():
+                wide[...] = jnp.zeros_like(wide)
+
+                def one(c, _):
+                    at = where_ref[base + c]
+
+                    @pl.when(at >= 0)
+                    def _():
+                        values = cold_ref[at].astype(jnp.float32)
+                        codes = jnp.clip(values / flat_step[...], -127.0, 127.0).astype(jnp.bfloat16)
+                        codes = codes.astype(jnp.float32)
+                        miss = values - codes * flat_step[...]
+                        flat_err[...] += miss * miss
+                        wide[pl.ds(c, rows, stride=capacity), :] = codes
+                    return 0
+
+                lax.fori_loop(0, capacity, one, 0)
+                for r in range(rows):
+                    out_ref[s, :, r * 128:(r + 1) * 128] = wide[r * capacity:(r + 1) * capacity, :].astype(jnp.bfloat16)
+
+        @pl.when(i == pl.num_programs(0) - 1)
+        def _():
+            for k in range(lines):
+                err_ref[0:1, k * 128:(k + 1) * 128] = jnp.sum(
+                    flat_err[pl.ds(k, quads, stride=lines), :], axis=0, keepdims=True)
+
+
+def finish(flag, where_held, arrived, cold, step_row, period, per_step=4):
+    sources, capacity, width = arrived.shape
+    rows = width // 128
+    smem = pl.BlockSpec(memory_space=pltpu.SMEM)
+    return pl.pallas_call(
+        functools.partial(finish_kernel, period),
+        grid=(sources // per_step,),
+        out_shape=(jax.ShapeDtypeStruct(arrived.shape, jnp.bfloat16),
+                   jax.ShapeDtypeStruct((capacity, period), jnp.float32),
+                   jax.ShapeDtypeStruct((1, period // 4), jnp.float32)),
+        in_specs=[smem, smem,
+                  pl.BlockSpec((per_step, capacity, width), lambda i: (i, 0, 0)),
+                  pl.BlockSpec(cold.shape, lambda i: (0, 0, 0)),
+                  pl.BlockSpec((8, period), lambda i: (0, 0))],
+        out_specs=(pl.BlockSpec((per_step, capacity, width), lambda i: (i, 0, 0)),
+                   pl.BlockSpec((capacity, period), lambda i: (0, 0)),
+                   pl.BlockSpec((1, period // 4), lambda i: (0, 0))),
+        scratch_shapes=[
+            pltpu.VMEM((rows * capacity, 128), jnp.float32),
+            pltpu.VMEM((rows, 128), jnp.float32),
+            pltpu.VMEM((rows, 128), jnp.float32),
+        ],
+    )(flag, where_held, arrived, cold, step_row)
 
 
 def body(block_pool, sel_index, sel_layer, counts):
     own_count = lax.axis_size("own")
     rep_count = lax.axis_size("rep")
-    capacity = sel_index.shape[0] // 4
+    layers = own_count // SLICES
+    n_select = sel_index.shape[0]
+    capacity = n_select // 4
     tokens = block_pool.shape[1]
     half = block_pool.shape[2] // SLICES
     period = 4 * half
-    parted = part(block_pool, sel_index, sel_layer, counts, own_count // SLICES, capacity)
     denominator = float(own_count * rep_count * capacity * tokens)
-    arrived = lax.all_to_all(parted, "own", split_axis=0, concat_axis=0, tiled=True)
-    top = jnp.max(peaks(arrived, period)[0].reshape(4, half), axis=0)
-    step = HEADROOM * jnp.maximum(top, 1.0) / 127.0
-    codes, err = encode(arrived, jnp.tile(step, 4)[None, :], period)
-    error = jnp.sum(totals(err)[0].reshape(4, half), axis=0)
-    return codes[None, None], step[None, :], (error / (step * step * denominator))[None, :]
+    hot, cold, table = open_exchange(block_pool, sel_index, sel_layer, counts, capacity)
+    fits, one, two, number, where_held, flag = plan(table, capacity, n_select - capacity)
+
+    def sparse():
+        arrived, landed, step_row = lax.switch(
+            sel_layer[0], [functools.partial(route, layer) for layer in range(layers)], one, two, number, hot, cold)
+        return finish(flag, where_held, arrived, landed, step_row, period)
+
+    def dense():
+        parted = part(block_pool, sel_index, sel_layer, counts, layers, capacity)
+        arrived = lax.all_to_all(parted, "own", split_axis=0, concat_axis=0, tiled=True)
+        top = jnp.max(peaks(arrived, period)[0].reshape(4, half), axis=0)
+        step = HEADROOM * jnp.maximum(top, 1.0) / 127.0
+        codes, err = encode(arrived, jnp.tile(step, 4)[None, :], period)
+        return codes, err, step[None, :]
+
+    codes, err, step = lax.cond(fits[0] == 1, sparse, dense)
+    return codes[None, None], step, totals(err, step, denominator)
 
 
 def solution(mesh):

time: 198 us -> 133 us (0.67)
  the two profiles are of different devices: /device:TPU:0 before, /device:TPU:4 now
where the time goes in v2:
time: 133 us; the launch traced here: 132 us
  Pallas kernels  128 us (96%)
  between operations  1.95 us (1%)
    pallas_call x1, Pallas kernels, route(): pl.pallas_call(functools.partial(route_kernel, layer), out_shape=(jax.Sha...  88.2 us
    pallas_call x1, Pallas kernels, open_exchange(): pl.pallas_call(functools.partial(open_kernel, half), out_shape=(jax.Shape...  16.2 us
    pallas_call x1, Pallas kernels, finish(): pl.pallas_call(functools.partial(finish_kernel, period), grid=(sources //...  13.4 us
    pallas_call x1, Pallas kernels, totals(): pl.pallas_call(functools.partial(total_kernel, denominator), out_shape=ja...  6.02 us
    pallas_call x1, Pallas kernels, plan(): pl.pallas_call(functools.partial(plan_kernel, capacity, n_cold), out_shap...  3.9 us

profile of v2, /device:TPU:4, one launch (start us, length us, event | category | flops | bytes accessed | tf_op | source)
XLA Modules:
  0.0 132.1 jit_solution(11797421182165551676)
XLA Ops:
  1.3 16.2 %shard_map.67 = (bf16[2,8,18432]{2,1,0:T(8,128)(2,1)S(1)}, bf16[2,24,144,128]{3,2,1,0:T(8,128)(2,1)S(1)}, s32[4,32,1,128]{3,2,1,0:T(1,128)}) custom-call(s32[32]{0:T(128)} %idx_ref.1, s32[32]{0:T(128)} %lay_ref.1, s32[1]{0:T(128)S(6)} %copy.62.cnt_ref, bf16[64,64,576]{2,1,0:T(8,128)(2,1)} %pool_ref.1), custom_call_target="tpu_custom_call" | custom-call | tf_op jit(solution)/shard_map/pallas_call | solution.py:355
  17.5 3.9 %shard_map.68 = (s32[1]{0:T(128)}, s32[80]{0:T(128)S(1)}, s32[64]{0:T(128)S(1)}, s32[4]{0:T(128)S(1)}, s32[256]{0:T(256)S(1)}, /*index=5*/s32[1]{0:T(128)}) custom-call(s32[4,32,1,128]{3,2,1,0:T(1,128)} %get-tuple-element.296.table_ref.rows_ref, s32[4,32,1,128]{3,2,1,0:T(1,128)} %get-tuple-element.296.table_ref.rows_ref), custom_call_target="tpu_custom_call" | custom-call | tf_op jit(solution)/shard_map/pallas_call | solution.py:483
  22.1 102.8 %conditional.2 = ((bf16[32,8,18432]{2,1,0:T(8,128)(2,1)}, f32[8,1152]{1,0:T(8,128)S(1)}, f32[1,288]{1,0:T(1,128)S(1)})) conditional(s32[]{:T(128)} %bitcast.1, (s32[32]{0:T(128)}, s32[32]{0:T(128)}, s32[1]{0:T(128)}, bf16[64,64,576]{2,1,0:T(8,128)(2,1)}) %tuple.63, (s32[32]{0:T(128)}, s32[80]{0:T(128)S(1)}, s32[64]{0:T(128)S(1)}, s32[4]{0:T(128)S(1)}, ...), branch_computations={%region_0.0_spmd, %region_2.0_spmd} | conditional | flops 1440 | bytes 18918180 | solution.py:874
  22.8 88.6 %conditional = ((bf16[32,8,18432]{2,1,0:T(8,128)(2,1)}, bf16[64,144,128]{2,1,0:T(8,128)(2,1)}, f32[8,1152]{1,0:T(8,128)S(1)})) conditional(s32[]{:T(128)} %bitcast, (s32[80]{0:T(128)S(1)}, s32[64]{0:T(128)S(1)}, s32[4]{0:T(128)S(1)}, bf16[2,8,18432]{2,1,0:T(8,128)(2,1)S(1)}, ...), branch_computations={%region_3.0_spmd, %region_4.0_spmd, %region_5.0_spmd, %region_6.0_... | conditional | bytes 8 | solution.py:862
  22.8 88.2 %branch_8_fun.1 = (bf16[32,8,18432]{2,1,0:T(8,128)(2,1)}, bf16[64,144,128]{2,1,0:T(8,128)(2,1)}, f32[8,1152]{1,0:T(8,128)S(1)}) custom-call(s32[80]{0:T(128)S(1)} %get-tuple-element.230.one_ref, s32[64]{0:T(128)S(1)} %get-tuple-element.231.two_ref, s32[4]{0:T(128)S(1)} %get-tuple-element.232.number_ref, bf16[2,8,18432]{2,1,0:T(8,128)(2,1)S(1)} %get-tuple-element.233.hot_ref, ...), custom_call_target="tpu_custom_call" | custom-call | tf_op jit(solution)/shard_map/cond/branch_1_fun/cond/branch_8_fun/pallas_call | solution.py:719
  111.4 13.4 %branch_1_fun.3 = (bf16[32,8,18432]{2,1,0:T(8,128)(2,1)}, f32[8,1152]{1,0:T(8,128)S(1)}, f32[1,288]{1,0:T(1,128)S(1)}) custom-call(s32[1]{0:T(128)} %get-tuple-element.270.flag_ref, s32[256]{0:T(256)S(1)} %get-tuple-element.271.where_ref, bf16[32,8,18432]{2,1,0:T(8,128)(2,1)} %get-tuple-element.278.x_ref, bf16[64,144,128]{2,1,0:T(8,128)(2,1)} %get-tuple-element.279.cold_ref, ...), custom_call_target="tpu_custom_call" | custom-call | tf_op jit(solution)/shard_map/cond/branch_1_fun/pallas_call | solution.py:827
  124.9 0.0 copy-start
  124.9 6.0 %shard_map.69 = f32[1,288]{1,0:T(1,128)} custom-call(f32[8,1152]{1,0:T(8,128)S(1)} %get-tuple-element.307.err_ref, f32[1,288]{1,0:T(1,128)S(1)} %get-tuple-element.366.step_ref), custom_call_target="tpu_custom_call" | custom-call | tf_op jit(solution)/shard_map/pallas_call | solution.py:232
  130.9 1.2 copy.63
  132.1 0.0 copy-done
Async XLA Ops:
  124.9 7.3 %copy-start = (f32[1,288]{1,0:T(1,128)}, f32[1,288]{1,0:T(1,128)S(1)}, u32[]{:S(2)}) copy-start(f32[1,288]{1,0:T(1,128)S(1)} %get-tuple-element.366.step_ref) | copy-start | bytes 3460
